TPU v7x, 32 devices: a whole 2x2x4 slice. The times are simulated.
32 devices in a mesh: row: 16 (over z, y, x), col: 2 (over core).
Axes of the slice: x: 2, y: 2, z: 4, core: 2. Of those that a mesh axis runs over, the one named last changes fastest.
Arguments:
- lanczos_now: float32 [1, 256, 1024], P(None, 'row', 'col'), may hold values from -80 to 80, as said below
- lanczos_prev: float32 [1, 256, 1024], P(None, 'row', 'col'), may hold values from -6 to 6
- beta_prev: float32 [1], replicated, may hold values from 0.3 to 1.5
- valence_energy: float32 [256], P('row'), may hold values from -1.5 to -0.5
- conduction_energy: float32 [1024], P('col'), may hold values from 0.5 to 2.5
- valence_panel: float32 [16384, 256], P(('row', 'col')), may hold values from -0.375 to 0.375
- conduction_panel: float32 [16384, 1024], P(('row', 'col')), may hold values from -0.1875 to 0.1875
- screened_coulomb: float32 [16384, 16384], P('row', 'col'), may hold values from -0.046875 to 0.046875
- bare_coulomb: float32 [16384, 16384], P('row', 'col'), may hold values from -0.046875 to 0.046875
Outputs:
- lanczos_next: float32 [1, 256, 1024], P(None, 'row', 'col')
- coefficients: float32 [1, 2], replicated
Inputs may be any that keep to these rules, and one draw needn't show every extreme that they name: `lanczos_now`: real entries; the vectors of a chain are not normalized.
All inputs are finite; a program needn't handle non-finite values.
Results may differ from a plain program's by a relative error of at most 0.0002.
Values sent between devices are 32-bit elements; how exact they have to be, the bound alone decides.
A program may use at most 192 MiB of HBM per device.

v0:
```python
import jax
import jax.numpy as jnp
from jax import lax
from jax.sharding import PartitionSpec as P

V = 256
C = 1024
precise = lax.Precision.HIGHEST
epsilon = 1e-06


def per_device(
    lanczos_now,
    lanczos_prev,
    beta_prev,
    valence_energy,
    conduction_energy,
    valence_panel,
    conduction_panel,
    screened_coulomb,
    bare_coulomb,
):
    column_points = screened_coulomb.shape[1]
    wider = lax.all_gather(lanczos_now, "col", axis=2, tiled=True)
    vectors = lax.all_gather(wider, "row", axis=1, tiled=True)
    products = jnp.einsum("pv,kvc->pkc", valence_panel, vectors, precision=precise)
    density = jnp.sum(products * conduction_panel[:, None, :], axis=2)
    pair_local = jnp.einsum("pc,kvc->pkv", conduction_panel, vectors, precision=precise)
    every_panel, every_density = (
        lax.all_gather(valence_panel, ("row", "col"), axis=0, tiled=True),
        lax.all_gather(density, ("row", "col"), axis=0, tiled=True),
    )
    first_point = lax.axis_index("col") * column_points
    panel = lax.dynamic_slice_in_dim(every_panel, first_point, column_points, 0)
    far_density = lax.dynamic_slice_in_dim(every_density, first_point, column_points, 0)
    pair_terms = (
        jnp.einsum(
            "mkv,nv->mkn",
            lax.all_gather(pair_local, "col", axis=0, tiled=True),
            panel,
            precision=precise,
        )
        * screened_coulomb[:, None, :]
    )
    screened = jnp.einsum("mkn,nv->mkv", pair_terms, panel, precision=precise)
    potential = jnp.dot(bare_coulomb, far_density, precision=precise)
    direct_rows, local_potential = (
        lax.psum_scatter(screened, "col", scatter_dimension=0, tiled=True),
        lax.psum_scatter(potential, "col", scatter_dimension=0, tiled=True),
    )
    weighted = local_potential[:, :, None] * conduction_panel[:, None, :]
    bare_term = jnp.einsum("pv,pkc->vkc", valence_panel, weighted, precision=precise)
    screened_term = jnp.einsum("mkv,mc->vkc", direct_rows, conduction_panel, precision=precise)
    band_rows = lax.psum_scatter(
        2.0 * bare_term - screened_term, "row", scatter_dimension=0, tiled=True
    )
    kernel_part = lax.psum_scatter(band_rows, "col", scatter_dimension=2, tiled=True)
    kernel_part = jnp.transpose(kernel_part, (1, 0, 2))
    gaps = conduction_energy[None, None, :] - valence_energy[None, :, None]
    image = gaps * lanczos_now + kernel_part
    inverse_size = 1.0 / (V * C)
    sum_qu, sum_qq = lax.psum(
        (
            jnp.sum(lanczos_now * image, axis=(1, 2)),
            jnp.sum(lanczos_now * lanczos_now, axis=(1, 2)),
        ),
        ("row", "col"),
    )
    coef_alpha = sum_qu * inverse_size / (sum_qq * inverse_size + epsilon)
    resid = (
        image - coef_alpha[:, None, None] * lanczos_now - beta_prev[:, None, None] * lanczos_prev
    )
    sum_ww = lax.psum(jnp.sum(resid * resid, axis=(1, 2)), ("row", "col"))
    mean_ww = sum_ww * inverse_size
    beta_next = jnp.sqrt(mean_ww + epsilon)
    return (resid / beta_next[:, None, None], jnp.stack([coef_alpha, beta_next], axis=1))


def solution(mesh):
    placed = (
        P(None, "row", "col"),
        P(None, "row", "col"),
        P(),
        P("row"),
        P("col"),
        P(("row", "col"), None),
        P(("row", "col"), None),
        P("row", "col"),
        P("row", "col"),
    )
    return jax.shard_map(
        per_device,
        mesh=mesh,
        in_specs=placed,
        out_specs=(P(None, "row", "col"), P()),
        check_vma=False,
    )
```

profile of v0, /device:TPU:0, one launch (start us, length us, event | category | flops | bytes accessed | tf_op | source)
XLA Modules:
  0.0 517.7 jit_solution(11263954735266079760)
XLA Ops:
  7.2 0.0 all-gather.7.cloned.1.call-start
  7.2 3.5 all_gather.15
  10.8 0.0 all-gather.7.cloned.1.call-update
  10.8 0.0 all-gather.11.cloned.1.call-start
  10.8 57.7 %all-gather.7.cloned.1.call-done = f32[1,256,1024]{2,1,0:T(8,128)} async-done(((f32[1,16,1024]{2,1,0:T(8,128)}), f32[1,256,1024]{2,1,0:T(8,128)}) %all-gather.7.cloned.1.call-update) | async-done | bytes 1048592 | tf_op jit(solution)/shard_map/all_gather | solution.py:25
  68.6 4.5 fusion.21
  73.1 0.0 all-gather.11.cloned.1.call-update
  73.1 0.0 all-gather.9.cloned.1.call-start
  73.2 0.7 all-gather.9.cloned.1.call-update
  73.8 0.0 reduce-scatter.10.cloned.1.call-start
  73.9 4.1 multiply_reduce_fusion
  78.0 39.9 %all-gather.2 = f32[32,1,512]{2,1,0:T(1,128)S(1)} all-gather(f32[1,1,512]{2,1,0:T(1,128)S(1)} %bitcast.62), channel_id=2, replica_groups=mesh['row'=16,'col'=2] {'row','col'}, dimensions={0}, use_global_device_ids=true | all-gather | bytes 67584 | tf_op jit(solution)/shard_map/all_gather | solution.py:31
  117.9 30.6 %convolution_bitcast_fusion.1 = f32[1024,1]{1,0:T(8,128)} fusion(f32[8192,1]{0,1:T(1,128)S(1)} %bitcast.57, f32[1024,8192]{1,0:T(8,128)} %param.17), kind=kOutput, calls=%fused_computation.15 | convolution fusion | flops 100663296 | bytes 33591296 | tf_op jit(solution)/shard_map/dot_general | solution.py:46
  148.4 0.0 reduce-scatter.10.cloned.1.call-update
  148.5 0.2 reduce-scatter.8.cloned.1.call-start
  148.7 0.0 all-gather.11.cloned.1.call-done
  148.7 51.1 %all-gather.9.cloned.1.call-done = f32[16384,256]{1,0:T(8,128)} async-done(((f32[512,256]{1,0:T(8,128)}), f32[16384,256]{1,0:T(8,128)}) %all-gather.9.cloned.1.call-update) | async-done | bytes 16777232 | tf_op jit(solution)/shard_map/all_gather | solution.py:30
  199.8 32.1 %fusion.3 = f32[1024,8192]{1,0:T(8,128)} fusion(f32[1024,256]{1,0:T(8,128)} %all-gather.11.cloned.1.call-done, f32[16384,256]{1,0:T(8,128)} %all-gather.9.cloned.1.call-done, s32[]{:T(128)S(6)} %select_n.4), kind=kOutput, calls=%fused_computation.4 | convolution fusion | flops 25769803776 | bytes 42991620 | tf_op jit(solution)/shard_map/mkv,nv->mkn/dot_general | solution.py:37
  231.9 33.1 %fusion.13 = f32[1024,1,256]{2,0,1:T(8,128)} fusion(f32[16384,256]{1,0:T(8,128)} %all-gather.9.cloned.1.call-done, s32[]{:T(128)S(6)} %select_n.4, f32[1024,8192]{1,0:T(8,128)} %fusion.3, f32[1024,8192]{1,0:T(8,128)} %param.16), kind=kOutput, calls=%fused_computation.13 | convolution fusion | flops 25778192384 | bytes 76546048 | tf_op jit(solution)/shard_map/mkn,nv->mkv/dot_general | solution.py:45
  265.0 0.0 reduce-scatter.8.cloned.1.call-update
  265.0 0.3 all-reduce.4.cloned.1.call-start
  265.3 0.0 reduce-scatter.10.cloned.1.call-done
  265.3 1.1 copy.43
  266.4 5.4 %reduce-scatter.8.cloned.1.call-done = f32[512,1,256]{2,0,1:T(8,128)} async-done(((f32[1024,1,256]{2,0,1:T(8,128)}), f32[512,1,256]{2,0,1:T(8,128)}) %reduce-scatter.8.cloned.1.call-update) | async-done | bytes 524304 | tf_op jit(solution)/shard_map/reduce_scatter | solution.py:48
  271.8 4.5 convolution_bitcast_fusion
  276.3 0.0 copy-done.1
  276.3 4.6 fusion.18
  280.9 3.6 copy.36
  284.5 0.0 all-reduce.4.cloned.1.call-update
  284.5 0.0 reduce-scatter.12.cloned.1.call-start
  284.6 0.6 dynamic-slice.1
  285.8 112.5 %all-reduce.4.cloned.1.call-done = f32[256,1,1024]{2,1,0:T(1,128)} async-done(((f32[256,1,1024]{2,1,0:T(1,128)}), f32[256,1,1024]{2,1,0:T(1,128)}) %all-reduce.4.cloned.1.call-update) | async-done | bytes 1048592
  398.3 0.8 constant_dynamic-slice_fusion
  399.2 5.9 %copy.44 = f32[16,1,1024]{1,0,2:T(8,128)} copy(f32[16,1,1024]{2,1,0:T(1,128)S(1)} %constant_dynamic-slice_fusion) | data formatting | bytes 131072
  405.0 6.5 %bitcast_reduce_fusion = f32[1024,16]{1,0:T(8,128)} fusion(f32[16,1,1024]{1,0,2:T(8,128)} %copy.44), kind=kLoop, calls=%fused_computation.2 | loop fusion | bytes 131072
  411.5 0.0 reduce-scatter.12.cloned.1.call-update
  412.2 0.0 copy-done.2
  412.2 0.6 multiply_reduce_fusion.2
  412.8 5.9 %reduce-scatter.12.cloned.1.call-done = f32[512,16]{1,0:T(8,128)} async-done(((f32[1024,16]{1,0:T(8,128)}), f32[512,16]{1,0:T(8,128)}) %reduce-scatter.12.cloned.1.call-update) | async-done | bytes 32784
  418.7 3.4 reshape_bitcast_fusion
  422.1 2.8 copy.45
  425.0 0.0 copy-done.5
  425.0 0.8 multiply_reduce_fusion.3
  425.8 40.6 %all-reduce.1 = (f32[1]{0:T(128)}, f32[1]{0:T(128)}) all-reduce(f32[1]{0:T(128)} %bitcast.15, f32[1]{0:T(128)} %bitcast.16), channel_id=1, replica_groups=mesh['row'=16,'col'=2] {'row','col'}, use_global_device_ids=true, to_apply=%region_6.0 | all-reduce | flops 2 | bytes 16 | tf_op jit(solution)/shard_map/psum | solution.py:62
  467.8 0.7 multiply_reduce_fusion.1
  468.5 40.5 %psum.23 = f32[1]{0:T(128)} all-reduce(f32[1]{0:T(128)} %bitcast.19), channel_id=1, replica_groups=mesh['row'=16,'col'=2] {'row','col'}, use_global_device_ids=true, to_apply=%region_10.0 | all-reduce | flops 1 | bytes 8 | tf_op jit(solution)/shard_map/psum | solution.py:73
  509.6 0.6 copy.40
  510.2 0.6 pad_maximum_fusion
  (13 shorter events, 0.0 us)
Async XLA Ops:
  7.2 61.4 %all-gather.7.cloned.1.call-start = ((), (), s32[]{:S(2)}) async-start(), calls=%async_computation.3 | async-start | bytes 1114112 | tf_op jit(solution)/shard_map/all_gather | solution.py:25
  10.8 137.9 %all-gather.11.cloned.1.call-start = ((), (), s32[]{:S(2)}) async-start(), calls=%async_computation.6 | async-start | bytes 1572864 | tf_op jit(solution)/shard_map/all_gather | solution.py:39
  73.1 126.7 %all-gather.9.cloned.1.call-start = ((), (), s32[]{:S(2)}) async-start(), calls=%async_computation.4 | async-start | bytes 17301504 | tf_op jit(solution)/shard_map/all_gather | solution.py:30
  73.8 191.5 %reduce-scatter.10.cloned.1.call-start = ((), (), s32[]{:S(2)}) async-start(), calls=%async_computation.7 | async-start | bytes 786432
  148.5 123.3 %reduce-scatter.8.cloned.1.call-start = ((), (), s32[]{:S(2)}) async-start(), calls=%async_computation.5 | async-start | bytes 1572864 | tf_op jit(solution)/shard_map/reduce_scatter | solution.py:48
  231.9 39.9 %copy-start = (f32[512,1024]{1,0:T(8,128)S(1)}, f32[512,1024]{1,0:T(8,128)}, u32[]{:S(2)}) copy-start(f32[512,1024]{1,0:T(8,128)} %param.15) | copy-start | bytes 6291460
  231.9 44.4 %copy-start.1 = (f32[512,256]{1,0:T(8,128)S(1)}, f32[512,256]{1,0:T(8,128)}, u32[]{:S(2)}) copy-start(f32[512,256]{1,0:T(8,128)} %param.14) | copy-start | bytes 1572868
  265.0 19.6 %copy-start.6 = (u32[32]{0:T(128)S(1)}, u32[32]{0:T(128)}, u32[]{:S(2)}) copy-start(u32[32]{0:T(128)} %constant.20) | copy-start | bytes 388
  265.0 133.3 %all-reduce.4.cloned.1.call-start = ((), (), s32[]{:S(2)}) async-start(), calls=%async_computation.9 | async-start | bytes 2097152
  284.5 134.2 %reduce-scatter.12.cloned.1.call-start = ((), (), s32[]{:S(2)}) async-start(), calls=%async_computation.8 | async-start | bytes 786432
  399.2 13.0 %copy-start.2 = (f32[1,16,512]{2,1,0:T(8,128)S(1)}, f32[1,16,512]{2,1,0:T(8,128)}, u32[]{:S(2)}) copy-start(f32[1,16,512]{2,1,0:T(8,128)} %param.9) | copy-start | bytes 98308
  405.0 20.0 %copy-start.4 = (f32[512]{0:T(512)S(1)}, f32[512]{0:T(512)}, u32[]{:S(2)}) copy-start(f32[512]{0:T(512)} %param.13) | copy-start | bytes 6148
  405.0 20.0 %copy-start.5 = (f32[16]{0:T(128)S(1)}, f32[16]{0:T(128)}, u32[]{:S(2)}) copy-start(f32[16]{0:T(128)} %param.12) | copy-start | bytes 196
  405.0 62.8 %copy-start.3 = (f32[1,16,512]{2,1,0:T(8,128)S(1)}, f32[1,16,512]{2,1,0:T(8,128)}, u32[]{:S(2)}) copy-start(f32[1,16,512]{2,1,0:T(8,128)} %param.10) | copy-start | bytes 98308
Sparse Core Ops, SparseCore 0:
  10.9 57.6 all-gather.6
  73.2 7.8 all-gather.10
  84.0 115.7 all-gather.8
  201.9 6.1 reduce-scatter.9
  265.1 6.5 reduce-scatter.7
  284.6 113.6 all-reduce.3
  411.7 6.9 reduce-scatter.11
where the time goes:
time: 518 us
  waiting for transfers between devices  233 us (45%)
  blocking collectives  125 us (24%)
  matrix products  113 us (22%)
  local copies, waits for them, and re-layouts  25.4 us (5%)
  between operations  17.6 us (3%)
    unnamed x10, waiting for transfers between devices  119 us
    all_gather x1, waiting for transfers between devices, per_device(): vectors = lax.all_gather(wider, 'row', axis=1, tiled=True)  57.7 us
    all_gather x1, waiting for transfers between devices, per_device(): lax.all_gather(valence_panel, ('row', 'col'), axis=0, tiled=True)  51.1 us
    psum x1, blocking collectives, per_device(): lax.psum((jnp.sum(lanczos_now * image, axis=(1, 2)), jnp.sum(lanczos_now...  40.6 us
    psum x1, blocking collectives, per_device(): sum_ww = lax.psum(jnp.sum(resid * resid, axis=(1, 2)), ('row', 'col'))  40.5 us
    all_gather x1, blocking collectives, per_device(): lax.all_gather(density, ('row', 'col'), axis=0, tiled=True)  39.9 us
    dot_general x1, matrix products, per_device(): screened = jnp.einsum('mkn,nv->mkv', pair_terms, panel, precision=precise)  33.1 us
    dot_general x1, matrix products, per_device(): jnp.einsum('mkv,nv->mkn', lax.all_gather(pair_local, 'col', axis=0, tiled...  32.1 us
  transfers between devices with their start and end apart: 7, of which 5 were waited for; matrix products, arithmetic and copies ran while one was open for 20% of the time, Pallas kernels for 0%

commit v1 on v0

--- a/solution.py
+++ b/solution.py
@@ -7,6 +7,16 @@
 C = 1024
 precise = lax.Precision.HIGHEST
 epsilon = 1e-06
+
+
+def pass_along(x, axis, dim):
+    size = lax.axis_size(axis)
+    block, pieces = (x, [x])
+    for _ in range(size - 1):
+        block = lax.ppermute(block, axis, [(i, (i + 1) % size) for i in range(size)])
+        pieces.insert(0, block)
+    line = jnp.concatenate(pieces, axis=dim)
+    return jnp.roll(line, (lax.axis_index(axis) + 1) * x.shape[dim], axis=dim)
 
 
 def per_device(
@@ -22,7 +32,7 @@
 ):
     column_points = screened_coulomb.shape[1]
     wider = lax.all_gather(lanczos_now, "col", axis=2, tiled=True)
-    vectors = lax.all_gather(wider, "row", axis=1, tiled=True)
+    vectors = pass_along(wider, "row", 1)
     products = jnp.einsum("pv,kvc->pkc", valence_panel, vectors, precision=precise)
     density = jnp.sum(products * conduction_panel[:, None, :], axis=2)
     pair_local = jnp.einsum("pc,kvc->pkv", conduction_panel, vectors, precision=precise)

time: 518 us -> 609 us (1.18); the launches traced: 518 us -> 602 us
  waiting for transfers between devices: 233 us -> 289 us
  matrix products: 113 us -> 139 us
    ppermute x0 -> x15, waiting for transfers between devices: none -> 117 us  [pass_along(): lax.ppermute(block, axis, [(i, (i + 1) % size) for i in range(size)])]
    all_gather x1 -> x0, waiting for transfers between devices: 57.7 us -> none  [per_device(): vectors = lax.all_gather(wider, 'row', axis=1, tiled=True)]
    dot_general x1, matrix products: 32.1 us -> 58.3 us  [per_device(): jnp.einsum('mkv,nv->mkn', lax.all_gather(pair_local, 'col', axis=0, tiled...]
    unnamed x22 -> x56, local copies, waits for them, and re-layouts: 21.8 us -> 25.4 us
    unnamed x10 -> x9, waiting for transfers between devices: 119 us -> 119 us
  transfers between devices with their start and end apart: 7 -> 21, of which waited for: 5 -> 19; matrix products, arithmetic and copies ran while one was open for 20% -> 22% of each run, Pallas kernels for 0% -> 0%
where the time goes in v1:
time: 609 us; the launch traced here: 602 us
  waiting for transfers between devices  289 us (47%)
  matrix products  139 us (23%)
  blocking collectives  121 us (20%)
  local copies, waits for them, and re-layouts  29 us (5%)
  between operations  18.2 us (3%)
    unnamed x9, waiting for transfers between devices  119 us
    ppermute x15, waiting for transfers between devices, pass_along(): lax.ppermute(block, axis, [(i, (i + 1) % size) for i in range(size)])  117 us
    dot_general x1, matrix products, per_device(): jnp.einsum('mkv,nv->mkn', lax.all_gather(pair_local, 'col', axis=0, tiled...  58.3 us
    all_gather x1, waiting for transfers between devices, per_device(): lax.all_gather(valence_panel, ('row', 'col'), axis=0, tiled=True)  47.2 us
    psum x1, blocking collectives, per_device(): lax.psum((jnp.sum(lanczos_now * image, axis=(1, 2)), jnp.sum(lanczos_now...  40.6 us
    psum x1, blocking collectives, per_device(): sum_ww = lax.psum(jnp.sum(resid * resid, axis=(1, 2)), ('row', 'col'))  40.4 us
    all_gather x1, blocking collectives, per_device(): lax.all_gather(density, ('row', 'col'), axis=0, tiled=True)  37.6 us
    dot_general x1, matrix products, per_device(): screened = jnp.einsum('mkn,nv->mkv', pair_terms, panel, precision=precise)  32.9 us
  transfers between devices with their start and end apart: 21, of which 19 were waited for; matrix products, arithmetic and copies ran while one was open for 22% of the time, Pallas kernels for 0%

profile of v1, /device:TPU:0, one launch (start us, length us, event | category | flops | bytes accessed | tf_op | source)
XLA Modules:
  0.0 602.1 jit_solution(9812892258527024276)
XLA Ops:
  7.2 2.2 all_gather.12
  9.4 2.8 collective-permute-start
  12.3 6.4 %collective-permute-done = f32[1,16,1024]{2,1,0:T(8,128)S(1)} collective-permute-done((f32[1,16,1024]{2,1,0:T(8,128)S(1)}, f32[1,16,1024]{2,1,0:T(8,128)S(1)}, u32[]{:S(2)}, u32[]{:S(2)}) %collective-permute-start) | collective-permute-done | bytes 65568 | tf_op jit(solution)/shard_map/ppermute | solution.py:16
  18.7 7.9 %collective-permute-done.1 = f32[1,16,1024]{2,1,0:T(8,128)S(1)} collective-permute-done((f32[1,16,1024]{2,1,0:T(8,128)S(1)}, f32[1,16,1024]{2,1,0:T(8,128)S(1)}, u32[]{:S(2)}, u32[]{:S(2)}) %collective-permute-start.1) | collective-permute-done | bytes 65568 | tf_op jit(solution)/shard_map/ppermute | solution.py:16
  26.5 7.9 %collective-permute-done.2 = f32[1,16,1024]{2,1,0:T(8,128)S(1)} collective-permute-done((f32[1,16,1024]{2,1,0:T(8,128)S(1)}, f32[1,16,1024]{2,1,0:T(8,128)S(1)}, u32[]{:S(2)}, u32[]{:S(2)}) %collective-permute-start.2) | collective-permute-done | bytes 65568 | tf_op jit(solution)/shard_map/ppermute | solution.py:16
  34.4 7.9 %collective-permute-done.3 = f32[1,16,1024]{2,1,0:T(8,128)S(1)} collective-permute-done((f32[1,16,1024]{2,1,0:T(8,128)S(1)}, f32[1,16,1024]{2,1,0:T(8,128)S(1)}, u32[]{:S(2)}, u32[]{:S(2)}) %collective-permute-start.3) | collective-permute-done | bytes 65568 | tf_op jit(solution)/shard_map/ppermute | solution.py:16
  42.2 7.9 %collective-permute-done.4 = f32[1,16,1024]{2,1,0:T(8,128)S(1)} collective-permute-done((f32[1,16,1024]{2,1,0:T(8,128)S(1)}, f32[1,16,1024]{2,1,0:T(8,128)S(1)}, u32[]{:S(2)}, u32[]{:S(2)}) %collective-permute-start.4) | collective-permute-done | bytes 65568 | tf_op jit(solution)/shard_map/ppermute | solution.py:16
  50.1 7.9 %collective-permute-done.5 = f32[1,16,1024]{2,1,0:T(8,128)S(1)} collective-permute-done((f32[1,16,1024]{2,1,0:T(8,128)S(1)}, f32[1,16,1024]{2,1,0:T(8,128)S(1)}, u32[]{:S(2)}, u32[]{:S(2)}) %collective-permute-start.5) | collective-permute-done | bytes 65568 | tf_op jit(solution)/shard_map/ppermute | solution.py:16
  58.0 8.1 %collective-permute-done.6 = f32[1,16,1024]{2,1,0:T(8,128)S(1)} collective-permute-done((f32[1,16,1024]{2,1,0:T(8,128)S(1)}, f32[1,16,1024]{2,1,0:T(8,128)S(1)}, u32[]{:S(2)}, u32[]{:S(2)}) %collective-permute-start.6) | collective-permute-done | bytes 65568 | tf_op jit(solution)/shard_map/ppermute | solution.py:16
  66.1 7.9 %collective-permute-done.7 = f32[1,16,1024]{2,1,0:T(8,128)S(1)} collective-permute-done((f32[1,16,1024]{2,1,0:T(8,128)S(1)}, f32[1,16,1024]{2,1,0:T(8,128)S(1)}, u32[]{:S(2)}, u32[]{:S(2)}) %collective-permute-start.7) | collective-permute-done | bytes 65568 | tf_op jit(solution)/shard_map/ppermute | solution.py:16
  73.9 7.9 %collective-permute-done.8 = f32[1,16,1024]{2,1,0:T(8,128)S(1)} collective-permute-done((f32[1,16,1024]{2,1,0:T(8,128)S(1)}, f32[1,16,1024]{2,1,0:T(8,128)S(1)}, u32[]{:S(2)}, u32[]{:S(2)}) %collective-permute-start.8) | collective-permute-done | bytes 65568 | tf_op jit(solution)/shard_map/ppermute | solution.py:16
  81.8 7.9 %collective-permute-done.9 = f32[1,16,1024]{2,1,0:T(8,128)S(1)} collective-permute-done((f32[1,16,1024]{2,1,0:T(8,128)S(1)}, f32[1,16,1024]{2,1,0:T(8,128)S(1)}, u32[]{:S(2)}, u32[]{:S(2)}) %collective-permute-start.9) | collective-permute-done | bytes 65568 | tf_op jit(solution)/shard_map/ppermute | solution.py:16
  89.7 7.9 %collective-permute-done.10 = f32[1,16,1024]{2,1,0:T(8,128)S(1)} collective-permute-done((f32[1,16,1024]{2,1,0:T(8,128)S(1)}, f32[1,16,1024]{2,1,0:T(8,128)S(1)}, u32[]{:S(2)}, u32[]{:S(2)}) %collective-permute-start.10) | collective-permute-done | bytes 65568 | tf_op jit(solution)/shard_map/ppermute | solution.py:16
  97.5 7.9 %collective-permute-done.11 = f32[1,16,1024]{2,1,0:T(8,128)S(1)} collective-permute-done((f32[1,16,1024]{2,1,0:T(8,128)S(1)}, f32[1,16,1024]{2,1,0:T(8,128)S(1)}, u32[]{:S(2)}, u32[]{:S(2)}) %collective-permute-start.11) | collective-permute-done | bytes 65568 | tf_op jit(solution)/shard_map/ppermute | solution.py:16
  105.4 8.2 %collective-permute-done.12 = f32[1,16,1024]{2,1,0:T(8,128)S(1)} collective-permute-done((f32[1,16,1024]{2,1,0:T(8,128)S(1)}, f32[1,16,1024]{2,1,0:T(8,128)S(1)}, u32[]{:S(2)}, u32[]{:S(2)}) %collective-permute-start.12) | collective-permute-done | bytes 65568 | tf_op jit(solution)/shard_map/ppermute | solution.py:16
  113.6 7.9 %collective-permute-done.13 = f32[1,16,1024]{2,1,0:T(8,128)S(1)} collective-permute-done((f32[1,16,1024]{2,1,0:T(8,128)S(1)}, f32[1,16,1024]{2,1,0:T(8,128)S(1)}, u32[]{:S(2)}, u32[]{:S(2)}) %collective-permute-start.13) | collective-permute-done | bytes 65568 | tf_op jit(solution)/shard_map/ppermute | solution.py:16
  121.5 7.9 %collective-permute-done.14 = f32[1,16,1024]{2,1,0:T(8,128)S(1)} collective-permute-done((f32[1,16,1024]{2,1,0:T(8,128)S(1)}, f32[1,16,1024]{2,1,0:T(8,128)S(1)}, u32[]{:S(2)}, u32[]{:S(2)}) %collective-permute-start.14) | collective-permute-done | bytes 65568 | tf_op jit(solution)/shard_map/ppermute | solution.py:16
  129.8 1.3 copy-done.2
  131.1 2.7 convolution_bitcast_fusion.2
  134.0 0.7 all-gather.6.cloned.1.call-update
  134.7 1.8 copy.38
  136.6 5.6 fusion.5
  142.1 37.6 %all-gather.2 = f32[32,1,512]{2,1,0:T(1,128)S(1)} all-gather(f32[1,1,512]{2,1,0:T(1,128)S(1)} %bitcast.67), channel_id=2, replica_groups=mesh['row'=16,'col'=2] {'row','col'}, dimensions={0}, use_global_device_ids=true | all-gather | bytes 67584 | tf_op jit(solution)/shard_map/all_gather | solution.py:41
  179.8 30.6 %convolution_bitcast_fusion.1 = f32[1024,1]{1,0:T(8,128)} fusion(f32[8192,1]{0,1:T(1,128)S(1)} %bitcast.63, f32[1024,8192]{1,0:T(8,128)} %param.17), kind=kOutput, calls=%fused_computation.16 | convolution fusion | flops 100663296 | bytes 33591296 | tf_op jit(solution)/shard_map/dot_general | solution.py:56
  210.4 0.0 reduce-scatter.8.cloned.1.call-start
  210.4 47.2 %all-gather.6.cloned.1.call-done = f32[16384,256]{1,0:T(8,128)} async-done(((f32[512,256]{1,0:T(8,128)}), f32[16384,256]{1,0:T(8,128)}) %all-gather.6.cloned.1.call-update) | async-done | bytes 16777232 | tf_op jit(solution)/shard_map/all_gather | solution.py:40
  257.7 58.3 %fusion.3 = f32[1024,8192]{1,0:T(8,128)} fusion(f32[1024,256]{0,1:T(8,128)} %all-gather.8.cloned.1.call-done, f32[16384,256]{1,0:T(8,128)} %all-gather.6.cloned.1.call-done, s32[]{:T(128)S(6)} %select_n.19), kind=kOutput, calls=%fused_computation.4 | convolution fusion | flops 25769803776 | bytes 42991620 | tf_op jit(solution)/shard_map/mkv,nv->mkn/dot_general | solution.py:47
  316.0 32.9 %fusion.14 = f32[1024,1,256]{2,0,1:T(8,128)} fusion(f32[16384,256]{1,0:T(8,128)} %all-gather.6.cloned.1.call-done, s32[]{:T(128)S(6)} %select_n.19, f32[1024,8192]{1,0:T(8,128)} %fusion.3, f32[1024,8192]{1,0:T(8,128)} %param.16), kind=kOutput, calls=%fused_computation.14 | convolution fusion | flops 25778192384 | bytes 76546048 | tf_op jit(solution)/shard_map/mkn,nv->mkv/dot_general | solution.py:55
  349.0 1.1 copy.47
  350.0 5.6 reduce-scatter.8.cloned.1.call-done
  355.7 4.5 convolution_bitcast_fusion
  360.2 4.5 fusion.19
  364.7 3.6 copy.40
  368.4 0.6 dynamic-slice.1
  369.7 112.4 %all-reduce.4.cloned.1.call-done = f32[256,1,1024]{2,1,0:T(1,128)} async-done(((f32[256,1,1024]{2,1,0:T(1,128)}), f32[256,1,1024]{2,1,0:T(1,128)}) %all-reduce.4.cloned.1.call-update) | async-done | bytes 1048592
  482.1 0.8 constant_dynamic-slice_fusion
  483.0 6.1 %copy.48 = f32[16,1,1024]{1,0,2:T(8,128)} copy(f32[16,1,1024]{2,1,0:T(1,128)S(1)} %constant_dynamic-slice_fusion) | data formatting | bytes 131072
  489.0 6.5 %bitcast_reduce_fusion = f32[1024,16]{1,0:T(8,128)} fusion(f32[16,1,1024]{1,0,2:T(8,128)} %copy.48), kind=kLoop, calls=%fused_computation.2 | loop fusion | bytes 131072
  496.2 0.7 multiply_reduce_fusion.1
  496.9 5.8 reduce-scatter.12.cloned.1.call-done
  502.7 3.5 reshape_bitcast_fusion
  506.1 2.9 copy.49
  509.0 0.8 multiply_reduce_fusion.2
  509.8 40.6 %all-reduce.1 = (f32[1]{0:T(128)}, f32[1]{0:T(128)}) all-reduce(f32[1]{0:T(128)} %bitcast.17, f32[1]{0:T(128)} %bitcast.18), channel_id=1, replica_groups=mesh['row'=16,'col'=2] {'row','col'}, use_global_device_ids=true, to_apply=%region_6.7 | all-reduce | flops 2 | bytes 16 | tf_op jit(solution)/shard_map/psum | solution.py:72
  551.8 0.7 multiply_reduce_fusion
  552.5 40.4 %psum.23 = f32[1]{0:T(128)} all-reduce(f32[1]{0:T(128)} %bitcast.21), channel_id=1, replica_groups=mesh['row'=16,'col'=2] {'row','col'}, use_global_device_ids=true, to_apply=%region_10.11 | all-reduce | flops 1 | bytes 8 | tf_op jit(solution)/shard_map/psum | solution.py:83
  593.6 0.6 copy.44
  594.2 0.6 pad_maximum_fusion
  (75 shorter events, 0.6 us)
Async XLA Ops:
  7.2 203.3 %all-gather.8.cloned.1.call-start = ((), (), s32[]{:S(2)}) async-start(), calls=%async_computation.5 | async-start | bytes 1572864 | tf_op jit(solution)/shard_map/all_gather | solution.py:49
  9.4 9.2 %collective-permute-start = (f32[1,16,1024]{2,1,0:T(8,128)S(1)}, f32[1,16,1024]{2,1,0:T(8,128)S(1)}, u32[]{:S(2)}, u32[]{:S(2)}) collective-permute-start(f32[1,16,1024]{2,1,0:T(8,128)S(1)} %all_gather.12), channel_id=1, source_target_pairs={{0,2},{2,4},{4,6},{6,8},{8,10},{10,12},{12,14},{14,16},{16,18},{18... | collective-permute-start | bytes 196616 | tf_op jit(solution)/shard_map/ppermute | solution.py:16
  18.6 7.9 %collective-permute-start.1 = (f32[1,16,1024]{2,1,0:T(8,128)S(1)}, f32[1,16,1024]{2,1,0:T(8,128)S(1)}, u32[]{:S(2)}, u32[]{:S(2)}) collective-permute-start(f32[1,16,1024]{2,1,0:T(8,128)S(1)} %collective-permute-done), channel_id=1, source_target_pairs={{0,2},{2,4},{4,6},{6,8},{8,10},{10,12},{12,14},{14,16},{16,18},{18... | collective-permute-start | bytes 196616 | tf_op jit(solution)/shard_map/ppermute | solution.py:16
  26.5 7.9 %collective-permute-start.2 = (f32[1,16,1024]{2,1,0:T(8,128)S(1)}, f32[1,16,1024]{2,1,0:T(8,128)S(1)}, u32[]{:S(2)}, u32[]{:S(2)}) collective-permute-start(f32[1,16,1024]{2,1,0:T(8,128)S(1)} %collective-permute-done.1), channel_id=1, source_target_pairs={{0,2},{2,4},{4,6},{6,8},{8,10},{10,12},{12,14},{14,16},{16,18},{18... | collective-permute-start | bytes 196616 | tf_op jit(solution)/shard_map/ppermute | solution.py:16
  34.4 7.9 %collective-permute-start.3 = (f32[1,16,1024]{2,1,0:T(8,128)S(1)}, f32[1,16,1024]{2,1,0:T(8,128)S(1)}, u32[]{:S(2)}, u32[]{:S(2)}) collective-permute-start(f32[1,16,1024]{2,1,0:T(8,128)S(1)} %collective-permute-done.2), channel_id=1, source_target_pairs={{0,2},{2,4},{4,6},{6,8},{8,10},{10,12},{12,14},{14,16},{16,18},{18... | collective-permute-start | bytes 196616 | tf_op jit(solution)/shard_map/ppermute | solution.py:16
  42.2 7.9 %collective-permute-start.4 = (f32[1,16,1024]{2,1,0:T(8,128)S(1)}, f32[1,16,1024]{2,1,0:T(8,128)S(1)}, u32[]{:S(2)}, u32[]{:S(2)}) collective-permute-start(f32[1,16,1024]{2,1,0:T(8,128)S(1)} %collective-permute-done.3), channel_id=1, source_target_pairs={{0,2},{2,4},{4,6},{6,8},{8,10},{10,12},{12,14},{14,16},{16,18},{18... | collective-permute-start | bytes 196616 | tf_op jit(solution)/shard_map/ppermute | solution.py:16
  50.1 7.9 %collective-permute-start.5 = (f32[1,16,1024]{2,1,0:T(8,128)S(1)}, f32[1,16,1024]{2,1,0:T(8,128)S(1)}, u32[]{:S(2)}, u32[]{:S(2)}) collective-permute-start(f32[1,16,1024]{2,1,0:T(8,128)S(1)} %collective-permute-done.4), channel_id=1, source_target_pairs={{0,2},{2,4},{4,6},{6,8},{8,10},{10,12},{12,14},{14,16},{16,18},{18... | collective-permute-start | bytes 196616 | tf_op jit(solution)/shard_map/ppermute | solution.py:16
  58.0 8.1 %collective-permute-start.6 = (f32[1,16,1024]{2,1,0:T(8,128)S(1)}, f32[1,16,1024]{2,1,0:T(8,128)S(1)}, u32[]{:S(2)}, u32[]{:S(2)}) collective-permute-start(f32[1,16,1024]{2,1,0:T(8,128)S(1)} %collective-permute-done.5), channel_id=1, source_target_pairs={{0,2},{2,4},{4,6},{6,8},{8,10},{10,12},{12,14},{14,16},{16,18},{18... | collective-permute-start | bytes 196616 | tf_op jit(solution)/shard_map/ppermute | solution.py:16
  66.1 7.9 %collective-permute-start.7 = (f32[1,16,1024]{2,1,0:T(8,128)S(1)}, f32[1,16,1024]{2,1,0:T(8,128)S(1)}, u32[]{:S(2)}, u32[]{:S(2)}) collective-permute-start(f32[1,16,1024]{2,1,0:T(8,128)S(1)} %collective-permute-done.6), channel_id=1, source_target_pairs={{0,2},{2,4},{4,6},{6,8},{8,10},{10,12},{12,14},{14,16},{16,18},{18... | collective-permute-start | bytes 196616 | tf_op jit(solution)/shard_map/ppermute | solution.py:16
  73.9 7.9 %collective-permute-start.8 = (f32[1,16,1024]{2,1,0:T(8,128)S(1)}, f32[1,16,1024]{2,1,0:T(8,128)S(1)}, u32[]{:S(2)}, u32[]{:S(2)}) collective-permute-start(f32[1,16,1024]{2,1,0:T(8,128)S(1)} %collective-permute-done.7), channel_id=1, source_target_pairs={{0,2},{2,4},{4,6},{6,8},{8,10},{10,12},{12,14},{14,16},{16,18},{18... | collective-permute-start | bytes 196616 | tf_op jit(solution)/shard_map/ppermute | solution.py:16
  81.8 7.9 %collective-permute-start.9 = (f32[1,16,1024]{2,1,0:T(8,128)S(1)}, f32[1,16,1024]{2,1,0:T(8,128)S(1)}, u32[]{:S(2)}, u32[]{:S(2)}) collective-permute-start(f32[1,16,1024]{2,1,0:T(8,128)S(1)} %collective-permute-done.8), channel_id=1, source_target_pairs={{0,2},{2,4},{4,6},{6,8},{8,10},{10,12},{12,14},{14,16},{16,18},{18... | collective-permute-start | bytes 196616 | tf_op jit(solution)/shard_map/ppermute | solution.py:16
  89.7 7.9 %collective-permute-start.10 = (f32[1,16,1024]{2,1,0:T(8,128)S(1)}, f32[1,16,1024]{2,1,0:T(8,128)S(1)}, u32[]{:S(2)}, u32[]{:S(2)}) collective-permute-start(f32[1,16,1024]{2,1,0:T(8,128)S(1)} %collective-permute-done.9), channel_id=1, source_target_pairs={{0,2},{2,4},{4,6},{6,8},{8,10},{10,12},{12,14},{14,16},{16,18},{18... | collective-permute-start | bytes 196616 | tf_op jit(solution)/shard_map/ppermute | solution.py:16
  97.5 7.9 %collective-permute-start.11 = (f32[1,16,1024]{2,1,0:T(8,128)S(1)}, f32[1,16,1024]{2,1,0:T(8,128)S(1)}, u32[]{:S(2)}, u32[]{:S(2)}) collective-permute-start(f32[1,16,1024]{2,1,0:T(8,128)S(1)} %collective-permute-done.10), channel_id=1, source_target_pairs={{0,2},{2,4},{4,6},{6,8},{8,10},{10,12},{12,14},{14,16},{16,18},{18... | collective-permute-start | bytes 196616 | tf_op jit(solution)/shard_map/ppermute | solution.py:16
  105.4 8.2 %collective-permute-start.12 = (f32[1,16,1024]{2,1,0:T(8,128)S(1)}, f32[1,16,1024]{2,1,0:T(8,128)S(1)}, u32[]{:S(2)}, u32[]{:S(2)}) collective-permute-start(f32[1,16,1024]{2,1,0:T(8,128)S(1)} %collective-permute-done.11), channel_id=1, source_target_pairs={{0,2},{2,4},{4,6},{6,8},{8,10},{10,12},{12,14},{14,16},{16,18},{18... | collective-permute-start | bytes 196616 | tf_op jit(solution)/shard_map/ppermute | solution.py:16
  113.6 7.9 %collective-permute-start.13 = (f32[1,16,1024]{2,1,0:T(8,128)S(1)}, f32[1,16,1024]{2,1,0:T(8,128)S(1)}, u32[]{:S(2)}, u32[]{:S(2)}) collective-permute-start(f32[1,16,1024]{2,1,0:T(8,128)S(1)} %collective-permute-done.12), channel_id=1, source_target_pairs={{0,2},{2,4},{4,6},{6,8},{8,10},{10,12},{12,14},{14,16},{16,18},{18... | collective-permute-start | bytes 196616 | tf_op jit(solution)/shard_map/ppermute | solution.py:16
  121.5 7.9 %collective-permute-start.14 = (f32[1,16,1024]{2,1,0:T(8,128)S(1)}, f32[1,16,1024]{2,1,0:T(8,128)S(1)}, u32[]{:S(2)}, u32[]{:S(2)}) collective-permute-start(f32[1,16,1024]{2,1,0:T(8,128)S(1)} %collective-permute-done.13), channel_id=1, source_target_pairs={{0,2},{2,4},{4,6},{6,8},{8,10},{10,12},{12,14},{14,16},{16,18},{18... | collective-permute-start | bytes 196616 | tf_op jit(solution)/shard_map/ppermute | solution.py:16
  121.5 9.7 %copy-start = (f32[512,1024]{1,0:T(8,128)S(1)}, f32[512,1024]{1,0:T(8,128)}, u32[]{:S(2)}) copy-start(f32[512,1024]{1,0:T(8,128)} %param.15) | copy-start | bytes 6291460
  129.8 1.3 copy-start.2
  133.9 123.8 %all-gather.6.cloned.1.call-start = ((), (), s32[]{:S(2)}) async-start(), calls=%async_computation.3 | async-start | bytes 17301504 | tf_op jit(solution)/shard_map/all_gather | solution.py:40
  134.7 214.3 %reduce-scatter.10.cloned.1.call-start = ((), (), s32[]{:S(2)}) async-start(), calls=%async_computation.6 | async-start | bytes 786432
  134.7 1.9 copy-start.1
  210.4 145.3 %reduce-scatter.8.cloned.1.call-start = ((), (), s32[]{:S(2)}) async-start(), calls=%async_computation.4 | async-start | bytes 1572864 | tf_op jit(solution)/shard_map/reduce_scatter | solution.py:58
  348.9 133.2 %all-reduce.4.cloned.1.call-start = ((), (), s32[]{:S(2)}) async-start(), calls=%async_computation.8 | async-start | bytes 2097152
  364.7 3.7 copy-start.7
  368.4 134.3 %reduce-scatter.12.cloned.1.call-start = ((), (), s32[]{:S(2)}) async-start(), calls=%async_computation.7 | async-start | bytes 786432
  489.0 7.1 %copy-start.3 = (f32[1,16,512]{2,1,0:T(8,128)S(1)}, f32[1,16,512]{2,1,0:T(8,128)}, u32[]{:S(2)}) copy-start(f32[1,16,512]{2,1,0:T(8,128)} %param.9) | copy-start | bytes 98308
  506.1 2.9 copy-start.5
  506.1 2.9 copy-start.6
  506.1 45.6 %copy-start.4 = (f32[1,16,512]{2,1,0:T(8,128)S(1)}, f32[1,16,512]{2,1,0:T(8,128)}, u32[]{:S(2)}) copy-start(f32[1,16,512]{2,1,0:T(8,128)} %param.10) | copy-start | bytes 98308
Sparse Core Ops, SparseCore 0:
  134.0 4.8 all-gather.7
  141.8 115.8 all-gather.5
  259.9 6.1 reduce-scatter.9
  349.0 6.5 reduce-scatter.7
  368.5 113.5 all-reduce.3
  495.6 6.9 reduce-scatter.11
